TPU v7x, 256 devices: a whole 4x4x8 slice. The times are simulated.
256 devices in a mesh: replica: 32 (over y, z), shard: 8 (over x, core).
Axes of the slice: x: 4, y: 4, z: 8, core: 2. Of those that a mesh axis runs over, the one named last changes fastest.
Arguments:
- outer_params: float32 [1024, 4096], P('shard'), may hold values from -6 to 6, as said below
- local_params: bfloat16 [32, 1024, 4096], P('replica', 'shard'), may hold values from -70 to 70
- momentum: float32 [1024, 4096], P('shard'), may hold values from -6 to 6
Outputs:
- params_next: float32 [1024, 4096], P('shard')
- momentum_next: float32 [1024, 4096], P('shard')
- block_scales: float32 [32, 1024], P(None, 'shard')
Inputs may be any that keep to these rules, and one draw needn't show every extreme that they name: `outer_params`: outer parameters of order one.
All inputs are finite; a program needn't handle non-finite values.
Results may differ from a plain program's by a relative error of at most 0.005.
Values may be sent and summed in bfloat16 or wider, within the bound.
A program may use at most 64 MiB of HBM per device.

v0:
```python
import math
import jax
import jax.numpy as jnp
from jax import lax
from jax.sharding import Mesh
from jax.sharding import PartitionSpec as P

BLOCK = 128
REPLICA = ("replica_0", "replica_1")
REPLICA_SHARD = ("replica_0", "replica_1", "shard_0", "shard_1")
SHARD = ("shard_0", "shard_1")
epsilon = 1e-06
clip_level = 0.5
outer_rate = 0.7
outer_decay = 0.9
grid_levels = 7.0


def copy_for_each(x, axis):
    copies = jnp.broadcast_to(x, (lax.axis_size(axis), *x.shape))
    return lax.all_to_all(copies, axis, split_axis=0, concat_axis=0, tiled=True)


def taken_together(x, axis):
    everything = copy_for_each(x, axis)
    return jnp.max(everything, axis=0)


def in_blocks(x, dim, devices):
    dims = x.shape
    pieces = x.reshape(*dims[:dim], devices, dims[dim] // devices, *dims[dim + 1 :])
    return jnp.moveaxis(pieces, dim, 0)


def summed_on_arrival(x, axis, dim):
    pieces = in_blocks(x, dim, lax.axis_size(axis))
    arrived = lax.all_to_all(pieces, axis, split_axis=0, concat_axis=0, tiled=True)
    return arrived.astype(jnp.float32).sum(axis=0)


def over_axes(x, axes):
    for axis in axes:
        x = lax.psum(x, axis)
    return x


def smooth_step(values):
    return values - jnp.sin(2.0 * math.pi * values) / (2.0 * math.pi)


def smooth_round(values):
    return smooth_step(smooth_step(values))


def block_max(values):
    return jnp.max(
        jnp.abs(values).reshape(values.shape[0], values.shape[1] // BLOCK, BLOCK), axis=2
    )


def per_device(outer_params, local_params, momentum):
    workers = lax.axis_size(REPLICA)
    row_count = outer_params.shape[0]
    col_count = outer_params.shape[1]
    deltas = outer_params - local_params[0].astype(jnp.float32)
    absmax = taken_together(block_max(deltas), REPLICA)
    spread_scale = jnp.repeat(absmax + epsilon, BLOCK, axis=1)
    encoded = smooth_round(grid_levels * deltas / spread_scale).astype(jnp.bfloat16)
    summed_rows = summed_on_arrival(
        (spread_scale * encoded.astype(jnp.float32) / grid_levels).astype(jnp.bfloat16), REPLICA, 0
    )
    gradient_slice = summed_rows / workers
    square_total = over_axes(jnp.sum(gradient_slice * gradient_slice), REPLICA_SHARD)
    entry_count = row_count * lax.axis_size(SHARD) * col_count
    root_mean = jnp.sqrt(square_total / entry_count + epsilon)
    factor = jnp.minimum(1.0, clip_level / root_mean)
    gradient = lax.all_gather(gradient_slice, REPLICA, axis=0, tiled=True)
    clipped = factor * gradient
    momentum_next = outer_decay * momentum + clipped
    params_next = outer_params - outer_rate * (clipped + outer_decay * momentum_next)
    return (params_next, momentum_next, absmax.T)


def solution(mesh):
    finer = Mesh(mesh.devices.reshape(4, 8, 4, 2), ("replica_0", "replica_1", "shard_0", "shard_1"))
    placed = (P(SHARD, None), P(REPLICA, SHARD, None), P(SHARD, None))
    return jax.shard_map(
        per_device,
        mesh=finer,
        in_specs=placed,
        out_specs=(P(SHARD, None), P(SHARD, None), P(None, SHARD)),
        check_vma=False,
    )
```

profile of v0, /device:TPU:2, one launch (start us, length us, event | category | flops | bytes accessed | tf_op | source)
XLA Modules:
  0.0 185.8 jit_solution(7357414329227839950)
XLA Ops:
  7.2 0.0 all-gather.3.cloned.1.call-start
  7.2 2.1 %abs_bitcast_fusion = f32[16,8,32,128]{3,1,2,0:T(8,128)S(1)} fusion(f32[128,4096]{1,0:T(8,128)} %param.3, bf16[1,128,4096]{2,1,0:T(8,128)(2,1)} %param.4), kind=kLoop, calls=%fused_computation.9 | loop fusion | flops 1572864 | bytes 5242880
  9.3 0.4 copy.10
  9.7 0.6 reduce_max.18
  10.3 0.1 copy.8
  10.4 0.0 copy-start
  10.4 0.0 copy-start.1
  10.4 0.1 broadcast_in_dim.6
  10.5 28.4 %all_to_all.10 = f32[32,128,32]{1,2,0:T(8,128)} all-to-all(f32[32,128,32]{1,2,0:T(8,128)S(1)} %broadcast_in_dim.6), channel_id=1, replica_groups=mesh['replica_0'=4,'replica_1'=8,'shard_0'=4,'shard_1'=2] {'replica_0','..., dimensions={0} | all-to-all | bytes 1048576 | tf_op jit(solution)/shard_map/all_to_all | solution.py:21
  38.8 1.1 reduce_max.19
  39.9 0.0 copy-start.2
  39.9 0.1 copy.9
  40.0 0.6 broadcast_in_dim.7
  40.6 0.0 copy-done
  40.6 0.0 copy-done.1
  40.6 15.7 %fusion.1 = bf16[128,4096]{1,0:T(8,128)(2,1)} fusion(f32[16,8,32,128]{3,2,1,0:T(8,128)S(1)} %bitcast.24, f32[128,4096]{1,0:T(8,128)S(1)} %copy-done, bf16[1,128,4096]{2,1,0:T(8,128)(2,1)S(1)} %copy-done.1), kind=kLoop, calls=%fused_computation.3 | loop fusion | flops 7864320 | bytes 6291456 | tf_op jit(solution)/shard_map/convert_element_type | solution.py:70
  56.4 0.0 copy-done.2
  56.4 1.5 reshape.19
  57.9 33.7 %all_to_all.11 = bf16[32,4,4096]{2,1,0:T(4,128)(2,1)S(1)} all-to-all(bf16[32,4,4096]{2,1,0:T(4,128)(2,1)S(1)} %reshape.19), channel_id=1, replica_groups=mesh['replica_0'=4,'replica_1'=8,'shard_0'=4,'shard_1'=2] {'replica_0','..., dimensions={0} | all-to-all | bytes 2097152 | tf_op jit(solution)/shard_map/all_to_all | solution.py:37
  91.5 0.4 convert_reduce_fusion
  92.0 1.2 multiply_reduce_fusion
  93.2 0.0 all-gather.3.cloned.1.call-update
  93.2 9.2 %psum.28 = f32[]{:T(128)} all-reduce(f32[]{:T(128)} %get-tuple-element.5), channel_id=1, replica_groups=mesh['replica_0'=4,'replica_1'=8,'shard_0'=4,'shard_1'=2] {'replica_0'}, use_global_device_ids=true, to_apply=%region_4.0 | all-reduce | flops 1 | bytes 8 | tf_op jit(solution)/shard_map/psum | solution.py:43
  102.4 16.8 %psum.29 = f32[]{:T(128)} all-reduce(f32[]{:T(128)} %psum.28), channel_id=1, replica_groups=mesh['replica_0'=4,'replica_1'=8,'shard_0'=4,'shard_1'=2] {'replica_1'}, use_global_device_ids=true, to_apply=%region_5.0 | all-reduce | flops 1 | bytes 8 | tf_op jit(solution)/shard_map/psum | solution.py:43
  119.2 9.2 %psum.30 = f32[]{:T(128)} all-reduce(f32[]{:T(128)} %psum.29), channel_id=1, replica_groups=mesh['replica_0'=4,'replica_1'=8,'shard_0'=4,'shard_1'=2] {'shard_0'}, use_global_device_ids=true, to_apply=%region_6.0 | all-reduce | flops 1 | bytes 8 | tf_op jit(solution)/shard_map/psum | solution.py:43
  128.4 3.1 %psum.31 = f32[]{:T(128)} all-reduce(f32[]{:T(128)} %psum.30), channel_id=1, replica_groups=mesh['replica_0'=4,'replica_1'=8,'shard_0'=4,'shard_1'=2] {'shard_1'}, use_global_device_ids=true, to_apply=%region_7.0 | all-reduce | flops 1 | bytes 8 | tf_op jit(solution)/shard_map/psum | solution.py:43
  132.2 35.7 %all-gather.3.cloned.1.call-done = f32[32,4,4096]{2,1,0:T(4,128)} async-done(((f32[1,4,4096]{2,1,0:T(4,128)}), f32[32,4,4096]{2,1,0:T(4,128)}) %all-gather.3.cloned.1.call-update) | async-done | bytes 2097168 | tf_op jit(solution)/shard_map/all_gather | solution.py:77
  167.9 3.1 %broadcast_multiply_fusion = f32[16,8,4096]{2,1,0:T(8,128)} fusion(f32[16,8,4096]{2,1,0:T(8,128)} %bitcast.27, f32[]{:T(128)S(6)} %min_shard_map.3), kind=kLoop, calls=%fused_computation.10 | loop fusion | flops 524288 | bytes 4194308 | tf_op jit(solution)/shard_map/mul | solution.py:78
  171.0 2.9 %reshape.24 = f32[128,4096]{1,0:T(8,128)} reshape(f32[32,4,4096]{2,1,0:T(4,128)} %bitcast.25) | data formatting | bytes 4194304 | tf_op jit(solution)/shard_map/mul | solution.py:78
  173.9 5.0 %multiply_subtract_fusion = (f32[128,4096]{1,0:T(8,128)}, f32[128,4096]{1,0:T(8,128)}) fusion(f32[128,4096]{1,0:T(8,128)S(1)} %copy-done, f32[128,4096]{1,0:T(8,128)} %reshape.24, f32[128,4096]{1,0:T(8,128)} %param.5), kind=kLoop, calls=%fused_computation.5 | loop fusion | flops 3145728 | bytes 10485760 | tf_op jit(solution)/shard_map/sub | solution.py:80
  (1 shorter events, 0.0 us)
Async XLA Ops:
  7.2 160.7 %all-gather.3.cloned.1.call-start = ((), (), s32[]{:S(2)}) async-start(), calls=%async_computation.2 | async-start | bytes 2162688 | tf_op jit(solution)/shard_map/all_gather | solution.py:77
  10.4 30.3 %copy-start = (f32[128,4096]{1,0:T(8,128)S(1)}, f32[128,4096]{1,0:T(8,128)}, u32[]{:S(2)}) copy-start(f32[128,4096]{1,0:T(8,128)} %param.3) | copy-start | bytes 6291460
  10.4 30.3 %copy-start.1 = (bf16[1,128,4096]{2,1,0:T(8,128)(2,1)S(1)}, bf16[1,128,4096]{2,1,0:T(8,128)(2,1)}, u32[]{:S(2)}) copy-start(bf16[1,128,4096]{2,1,0:T(8,128)(2,1)} %param.4) | copy-start | bytes 3145732
  39.9 16.5 %copy-start.2 = (f32[128,32]{0,1:T(8,128)}, f32[128,32]{0,1:T(8,128)S(1)}, u32[]{:S(2)}) copy-start(f32[128,32]{0,1:T(8,128)S(1)} %reduce_max.19) | copy-start | bytes 49156
Sparse Core Ops, SparseCore 0:
  93.4 74.4 all-gather.2
where the time goes:
time: 186 us
  blocking collectives  100 us (54%)
  waiting for transfers between devices  35.7 us (19%)
  other arithmetic  29.4 us (16%)
  between operations  14.8 us (8%)
  local copies, waits for them, and re-layouts  5.59 us (3%)
    psum x4, blocking collectives, over_axes(): x = lax.psum(x, axis)  38.2 us
    all_gather x1, waiting for transfers between devices, per_device(): gradient = lax.all_gather(gradient_slice, REPLICA, axis=0, tiled=True)  35.7 us
    all_to_all x1, blocking collectives, summed_on_arrival(): lax.all_to_all(pieces, axis, split_axis=0, concat_axis=0, tiled=True)  33.7 us
    all_to_all x1, blocking collectives, copy_for_each(): return lax.all_to_all(copies, axis, split_axis=0, concat_axis=0, tiled=True)  28.4 us
    convert_element_type x1, other arithmetic, per_device(): (spread_scale * encoded.astype(jnp.float32) / grid_levels).astype(jnp.bfl...  15.7 us
    sub x1, other arithmetic, per_device(): outer_params - outer_rate * (clipped + outer_decay * momentum_next)  5.05 us
  transfers between devices with their start and end apart: 1, of which 1 were waited for; matrix products, arithmetic and copies ran while one was open for 0% of the time, Pallas kernels for 0%

commit v1 on v0

--- a/solution.py
+++ b/solution.py
@@ -74,7 +74,8 @@
     entry_count = row_count * lax.axis_size(SHARD) * col_count
     root_mean = jnp.sqrt(square_total / entry_count + epsilon)
     factor = jnp.minimum(1.0, clip_level / root_mean)
-    gradient = lax.all_gather(gradient_slice, REPLICA, axis=0, tiled=True)
+    repeated = jnp.stack([gradient_slice] * lax.axis_size(REPLICA))
+    gradient = jnp.concatenate(lax.all_to_all(repeated, REPLICA, 0, 0), axis=0)
     clipped = factor * gradient
     momentum_next = outer_decay * momentum + clipped
     params_next = outer_params - outer_rate * (clipped + outer_decay * momentum_next)

time: 186 us -> 178 us (0.957); the launches traced: 186 us -> 174 us
  waiting for transfers between devices: 35.7 us -> 0.01 us
  blocking collectives: 100 us -> 132 us
  between operations: 14.8 us -> 1.41 us
  starting transfers between devices: 0.04 us -> 5.04 us
    all_gather x1 -> x0, waiting for transfers between devices: 35.7 us -> none  [per_device(): gradient = lax.all_gather(gradient_slice, REPLICA, axis=0, tiled=True)]
    psum x4, blocking collectives: 38.2 us -> 69.6 us  [over_axes(): x = lax.psum(x, axis)]
    all_to_all x0 -> x1, starting transfers between devices: none -> 5.04 us  [per_device(): gradient = jnp.concatenate(lax.all_to_all(repeated, REPLICA, 0, 0), axis=0)]
  transfers between devices with their start and end apart: 1 -> 1, of which waited for: 1 -> 0; matrix products, arithmetic and copies ran while one was open for 0% -> 0% of each run, Pallas kernels for 0% -> 0%
where the time goes in v1:
time: 178 us; the launch traced here: 174 us
  blocking collectives  132 us (74%)
  other arithmetic  28.6 us (16%)
  local copies, waits for them, and re-layouts  7.38 us (4%)
  starting transfers between devices  5.04 us (3%)
    psum x4, blocking collectives, over_axes(): x = lax.psum(x, axis)  69.6 us
    all_to_all x1, blocking collectives, summed_on_arrival(): lax.all_to_all(pieces, axis, split_axis=0, concat_axis=0, tiled=True)  33.7 us
    all_to_all x1, blocking collectives, copy_for_each(): return lax.all_to_all(copies, axis, split_axis=0, concat_axis=0, tiled=True)  28.4 us
    convert_element_type x1, other arithmetic, per_device(): (spread_scale * encoded.astype(jnp.float32) / grid_levels).astype(jnp.bfl...  15.7 us
    all_to_all x1, starting transfers between devices, per_device(): gradient = jnp.concatenate(lax.all_to_all(repeated, REPLICA, 0, 0), axis=0)  5.04 us
    sub x1, other arithmetic, per_device(): outer_params - outer_rate * (clipped + outer_decay * momentum_next)  4.86 us
  transfers between devices with their start and end apart: 1, of which 0 were waited for; matrix products, arithmetic and copies ran while one was open for 0% of the time, Pallas kernels for 0%

profile of v1, /device:TPU:2, one launch (start us, length us, event | category | flops | bytes accessed | tf_op | source)
XLA Modules:
  0.0 174.1 jit_solution(10618491171491076700)
XLA Ops:
  0.6 2.1 %abs_bitcast_fusion = f32[16,8,32,128]{3,1,2,0:T(8,128)S(1)} fusion(f32[128,4096]{1,0:T(8,128)} %param.3, bf16[1,128,4096]{2,1,0:T(8,128)(2,1)} %param.4), kind=kLoop, calls=%fused_computation.9 | loop fusion | flops 1572864 | bytes 5242880
  2.7 0.4 copy.10
  3.1 0.6 reduce_max.18
  3.7 0.1 copy.8
  3.8 0.0 copy-start
  3.8 0.0 copy-start.1
  3.8 0.1 broadcast_in_dim.6
  3.9 28.4 %all_to_all.15 = f32[32,128,32]{1,2,0:T(8,128)} all-to-all(f32[32,128,32]{1,2,0:T(8,128)S(1)} %broadcast_in_dim.6), channel_id=1, replica_groups=mesh['replica_0'=4,'replica_1'=8,'shard_0'=4,'shard_1'=2] {'replica_0','..., dimensions={0} | all-to-all | bytes 1048576 | tf_op jit(solution)/shard_map/all_to_all | solution.py:21
  32.2 1.1 reduce_max.19
  33.3 0.0 copy-start.2
  33.3 0.1 copy.9
  33.4 0.6 broadcast_in_dim.7
  34.0 0.0 copy-done
  34.1 0.0 copy-done.1
  34.1 15.7 %fusion.1 = bf16[128,4096]{1,0:T(8,128)(2,1)} fusion(f32[16,8,32,128]{3,2,1,0:T(8,128)S(1)} %bitcast.22, f32[128,4096]{1,0:T(8,128)S(1)} %copy-done, bf16[1,128,4096]{2,1,0:T(8,128)(2,1)S(1)} %copy-done.1), kind=kLoop, calls=%fused_computation.3 | loop fusion | flops 7864320 | bytes 6291456 | tf_op jit(solution)/shard_map/convert_element_type | solution.py:70
  49.8 0.0 copy-done.2
  49.8 1.5 reshape.24
  51.3 33.7 %all_to_all.16 = bf16[32,4,4096]{2,1,0:T(4,128)(2,1)S(1)} all-to-all(bf16[32,4,4096]{2,1,0:T(4,128)(2,1)S(1)} %reshape.24), channel_id=1, replica_groups=mesh['replica_0'=4,'replica_1'=8,'shard_0'=4,'shard_1'=2] {'replica_0','..., dimensions={0} | all-to-all | bytes 2097152 | tf_op jit(solution)/shard_map/all_to_all | solution.py:37
  85.0 0.4 convert_reduce_fusion
  85.4 0.6 multiply_reduce_fusion
  86.0 1.8 %stack.2 = f32[32,4,4096]{2,1,0:T(4,128)} broadcast(f32[4,4096]{1,0:T(4,128)S(1)} %get-tuple-element.6), dimensions={1,2} | broadcast | bytes 2162688 | tf_op jit(solution)/shard_map/stack | solution.py:77
  87.8 5.0 %all-to-all-start.2 = ((f32[32,4,4096]{2,1,0:T(4,128)}), f32[32,4,4096]{2,1,0:T(4,128)}, u32[]{:S(2)}, u32[]{:S(2)}) async-start(f32[32,4,4096]{2,1,0:T(4,128)} %stack.2), calls=%async_computation.2 | async-start | bytes 4194304 | tf_op jit(solution)/shard_map/all_to_all | solution.py:78
  92.9 11.8 %psum.28 = f32[]{:T(128)} all-reduce(f32[]{:T(128)} %get-tuple-element.5), channel_id=1, replica_groups=mesh['replica_0'=4,'replica_1'=8,'shard_0'=4,'shard_1'=2] {'replica_0'}, use_global_device_ids=true, to_apply=%region_4.0 | all-reduce | flops 1 | bytes 8 | tf_op jit(solution)/shard_map/psum | solution.py:43
  104.6 45.5 %psum.29 = f32[]{:T(128)} all-reduce(f32[]{:T(128)} %psum.28), channel_id=1, replica_groups=mesh['replica_0'=4,'replica_1'=8,'shard_0'=4,'shard_1'=2] {'replica_1'}, use_global_device_ids=true, to_apply=%region_5.0 | all-reduce | flops 1 | bytes 8 | tf_op jit(solution)/shard_map/psum | solution.py:43
  150.2 9.2 %psum.30 = f32[]{:T(128)} all-reduce(f32[]{:T(128)} %psum.29), channel_id=1, replica_groups=mesh['replica_0'=4,'replica_1'=8,'shard_0'=4,'shard_1'=2] {'shard_0'}, use_global_device_ids=true, to_apply=%region_6.0 | all-reduce | flops 1 | bytes 8 | tf_op jit(solution)/shard_map/psum | solution.py:43
  159.4 3.1 %psum.31 = f32[]{:T(128)} all-reduce(f32[]{:T(128)} %psum.30), channel_id=1, replica_groups=mesh['replica_0'=4,'replica_1'=8,'shard_0'=4,'shard_1'=2] {'shard_1'}, use_global_device_ids=true, to_apply=%region_7.0 | all-reduce | flops 1 | bytes 8 | tf_op jit(solution)/shard_map/psum | solution.py:43
  163.2 0.0 all-to-all-done.2
  163.2 3.1 %broadcast_multiply_fusion = f32[16,8,4096]{2,1,0:T(8,128)} fusion(f32[16,8,4096]{2,1,0:T(8,128)} %bitcast.20, f32[]{:T(128)S(6)} %min_shard_map.3), kind=kLoop, calls=%fused_computation.10 | loop fusion | flops 524288 | bytes 4194308 | tf_op jit(solution)/shard_map/mul | solution.py:79
  166.3 2.9 %mul.43 = f32[128,4096]{1,0:T(8,128)} reshape(f32[32,4,4096]{2,1,0:T(4,128)} %bitcast.23) | data formatting | bytes 4194304 | tf_op jit(solution)/shard_map/mul | solution.py:79
  169.2 4.9 %multiply_subtract_fusion = (f32[128,4096]{1,0:T(8,128)}, f32[128,4096]{1,0:T(8,128)}) fusion(f32[128,4096]{1,0:T(8,128)S(1)} %copy-done, f32[128,4096]{1,0:T(8,128)} %mul.43, f32[128,4096]{1,0:T(8,128)} %param.5), kind=kLoop, calls=%fused_computation.5 | loop fusion | flops 3145728 | bytes 10485760 | tf_op jit(solution)/shard_map/sub | solution.py:81
  (1 shorter events, 0.0 us)
Async XLA Ops:
  3.8 30.3 %copy-start = (f32[128,4096]{1,0:T(8,128)S(1)}, f32[128,4096]{1,0:T(8,128)}, u32[]{:S(2)}) copy-start(f32[128,4096]{1,0:T(8,128)} %param.3) | copy-start | bytes 6291460
  3.8 30.3 %copy-start.1 = (bf16[1,128,4096]{2,1,0:T(8,128)(2,1)S(1)}, bf16[1,128,4096]{2,1,0:T(8,128)(2,1)}, u32[]{:S(2)}) copy-start(bf16[1,128,4096]{2,1,0:T(8,128)(2,1)} %param.4) | copy-start | bytes 3145732
  33.3 16.5 %copy-start.2 = (f32[128,32]{0,1:T(8,128)}, f32[128,32]{0,1:T(8,128)S(1)}, u32[]{:S(2)}) copy-start(f32[128,32]{0,1:T(8,128)S(1)} %reduce_max.19) | copy-start | bytes 49156
  87.8 75.3 %all-to-all-start.2 = ((f32[32,4,4096]{2,1,0:T(4,128)}), f32[32,4,4096]{2,1,0:T(4,128)}, u32[]{:S(2)}, u32[]{:S(2)}) async-start(f32[32,4,4096]{2,1,0:T(4,128)} %stack.2), calls=%async_computation.2 | async-start | bytes 4194304 | tf_op jit(solution)/shard_map/all_to_all | solution.py:78
